TPU v7x, 32 devices: a whole 2x2x4 slice. The times are simulated.
32 devices in a mesh: groups: 2 (over y), slab: 4 (over z), pencil: 2 (over x), comp: 2 (over core).
Axes of the slice: x: 2, y: 2, z: 4, core: 2. Of those that a mesh axis runs over, the one named last changes fastest.
Arguments:
- u_start: float32 [3, 64, 64, 512], P(None, ('groups', 'slab'), 'pencil', 'comp'), parts along dimension 1, may hold values from -6 to 6
- toughness: float32 [64, 64, 512], P(('groups', 'slab'), 'pencil', 'comp'), parts along dimension 0, may hold values from 0.3 to 1.5
- crack_label: int32 [64, 64, 512], P(('groups', 'slab'), 'pencil', 'comp'), parts along dimension 0, may hold values from 0 to 2
- obs_weight: bfloat16 [32, 64, 2, 4096], P('slab', 'pencil', 'comp'), may hold values from -0.75 to 0.75
- sensor_cell: int32 [4096], replicated, may hold values from 0 to 4095
Outputs:
- moved: float32 [3, 64, 64, 512], P(None, ('groups', 'slab'), 'pencil', 'comp'), parts along dimension 1
- damage: float32 [64, 64, 512], P(('groups', 'slab'), 'pencil', 'comp'), parts along dimension 0
- readings: float32 [3, 8192], P(None, 'groups'), parts along dimension 1
There are 2 independent parts, one for each index of `groups`. A program takes and returns all parts, laid end to end along the dimension named above; an argument that names none is the same for every part. Nothing has to cross between parts.
Inputs may be any that keep to these rules, and one draw needn't show every extreme that they name: `sensor_cell`: numbers cell blocks as (64 z + y) * 2 + h. `crack_label`: 0 intact, 1 partly cracked, 2 cracked.
All inputs are finite; a program needn't handle non-finite values.
Results may differ from a plain program's by a relative error of at most 0.003.
Values sent between devices are 32-bit elements; how exact they have to be, the bound alone decides.
A program may use at most 128 MiB of HBM per device.

v0:
```python
import jax
import jax.numpy as jnp
from jax import lax
from jax.sharding import PartitionSpec as P

SHEAR_MODULUS = 1.0
LAME_FIRST = 1.5
RESIDUAL_STIFF = 0.001
TIME_DISP = 0.15
TIME_DAMAGE = 0.08
LENGTH_SCALE = 1.0
DAMAGE_LEVEL = 0.45
POINT_GAIN = 8.0


def with_halo(block, sides, width):
    for axis, dim in sides:
        count = lax.axis_size(axis)
        forward = [(i, i + 1) for i in range(count - 1)]
        backward = [(target, source) for source, target in forward]
        low = lax.ppermute(
            lax.slice_in_dim(block, block.shape[dim] - width, None, axis=dim), axis, forward
        )
        high = lax.ppermute(lax.slice_in_dim(block, 0, width, axis=dim), axis, backward)
        block = jnp.concatenate([low, block, high], axis=dim)
    return block


def central(source, spatial):
    if spatial == 0:
        return 0.5 * (source[..., 2:, 1:-1, 1:-1] - source[..., :-2, 1:-1, 1:-1])
    if spatial == 1:
        return 0.5 * (source[..., 1:-1, 2:, 1:-1] - source[..., 1:-1, :-2, 1:-1])
    return 0.5 * (source[..., 1:-1, 1:-1, 2:] - source[..., 1:-1, 1:-1, :-2])


def shrink(source):
    return source[..., 1:-1, 1:-1, 1:-1]


def laplace(source):
    return (
        source[2:, 1:-1, 1:-1]
        + source[:-2, 1:-1, 1:-1]
        + source[1:-1, 2:, 1:-1]
        + source[1:-1, :-2, 1:-1]
        + source[1:-1, 1:-1, 2:]
        + source[1:-1, 1:-1, :-2]
        - 6.0 * source[1:-1, 1:-1, 1:-1]
    )


def entry_key(first, second):
    return (min(first, second), max(first, second))


def rotate(matrix, first, second):
    other = 3 - first - second
    diag_first = matrix[first, first]
    diag_second = matrix[second, second]
    coupling = matrix[first, second]
    angle = 0.5 * jnp.arctan2(2.0 * coupling, diag_second - diag_first)
    cosine = jnp.cos(angle)
    sine = jnp.sin(angle)
    side_first = matrix[entry_key(other, first)]
    side_second = matrix[entry_key(other, second)]
    result = dict(matrix)
    result[first, first] = (
        cosine * cosine * diag_first - 2.0 * cosine * sine * coupling + sine * sine * diag_second
    )
    result[second, second] = (
        sine * sine * diag_first + 2.0 * cosine * sine * coupling + cosine * cosine * diag_second
    )
    result[first, second] = jnp.zeros_like(coupling)
    result[entry_key(other, first)] = cosine * side_first - sine * side_second
    result[entry_key(other, second)] = sine * side_first + cosine * side_second
    return result


def eigenvalues(matrix):
    for sweep_index in range(5):
        for first, second in ((0, 1), (0, 2), (1, 2)):
            matrix = rotate(matrix, first, second)
    return [matrix[0, 0], matrix[1, 1], matrix[2, 2]]


def advance(padded_disp, padded_damage, toughness):
    gradient = [
        [central(padded_disp[component], direction) for direction in range(3)]
        for component in range(3)
    ]
    strain = {}
    for first in range(3):
        for second in range(first, 3):
            strain[first, second] = 0.5 * (gradient[first][second] + gradient[second][first])
    trace_full = strain[0, 0] + strain[1, 1] + strain[2, 2]
    damage_mid = shrink(padded_damage)
    degrade = (1.0 - damage_mid) ** 2 + RESIDUAL_STIFF
    divergence = []
    for component in range(3):
        total_force = 0.0
        for direction in range(3):
            stress = 2.0 * SHEAR_MODULUS * strain[entry_key(component, direction)]
            if component == direction:
                stress = stress + LAME_FIRST * trace_full
            total_force = total_force + central(degrade * stress, direction)
        divergence.append(total_force)
    moved = shrink(shrink(padded_disp)) + TIME_DISP * jnp.stack(divergence)
    inner = {key_pair: shrink(entry_value) for key_pair, entry_value in strain.items()}
    trace_inner = shrink(trace_full)
    energy = 0.5 * LAME_FIRST * jnp.maximum(trace_inner, 0.0) ** 2
    for eigen_value in eigenvalues(inner):
        energy = energy + SHEAR_MODULUS * jnp.maximum(eigen_value, 0.0) ** 2
    damage_core = shrink(damage_mid)
    damage = damage_core + TIME_DAMAGE * (
        2.0 * (1.0 - damage_core) * energy
        - toughness / LENGTH_SCALE * damage_core
        + toughness * LENGTH_SCALE * laplace(damage_mid)
    )
    return (moved, damage)


def local(u_start, toughness, crack_label, obs_weight, sensor_cell):
    planes, rows, columns = toughness.shape
    damage = DAMAGE_LEVEL * crack_label.astype(jnp.float32)
    moved = u_start
    for repeat in range(2):
        stacked = jnp.concatenate([moved, damage[None]], axis=0)
        padded = with_halo(stacked, (("slab", 1), ("pencil", 2), ("comp", 3)), 2)
        moved, damage = advance(padded[:3], padded[3], toughness)
    pooled = jnp.mean(moved, axis=-1).reshape(3, planes * rows).astype(jnp.bfloat16)
    weight_rows = obs_weight.reshape(planes * rows, obs_weight.shape[-1])
    dense = jnp.dot(pooled, weight_rows, preferred_element_type=jnp.float32)
    plane_ids = lax.axis_index("slab") * planes + jnp.arange(planes, dtype=jnp.int32)
    row_ids = lax.axis_index("pencil") * rows + jnp.arange(rows, dtype=jnp.int32)
    block_ids = (
        (plane_ids[:, None] * (rows * lax.axis_size("pencil")) + row_ids[None, :])
        * lax.axis_size("comp")
        + lax.axis_index("comp")
    ).reshape(planes * rows)
    picks = (block_ids[:, None] == sensor_cell[None, :]).astype(jnp.bfloat16)
    point = jnp.dot(pooled, picks, preferred_element_type=jnp.float32)
    partial_sum = dense + POINT_GAIN * point
    readings = lax.psum(partial_sum, ("slab", "pencil", "comp"))
    return (moved, damage, readings)


def solution(mesh):
    return jax.shard_map(
        local,
        mesh=mesh,
        in_specs=(
            P(None, ("groups", "slab"), "pencil", "comp"),
            P(("groups", "slab"), "pencil", "comp"),
            P(("groups", "slab"), "pencil", "comp"),
            P("slab", "pencil", "comp", None),
            P(),
        ),
        out_specs=(
            P(None, ("groups", "slab"), "pencil", "comp"),
            P(("groups", "slab"), "pencil", "comp"),
            P(None, "groups"),
        ),
        check_vma=False,
    )
```

profile of v0, /device:TPU:0, one launch (start us, length us, event | category | flops | bytes accessed | tf_op | source)
XLA Modules:
  0.0 226.6 jit_solution(18250146474018214217)
XLA Ops:
  2.9 5.0 %collective-permute-start = (f32[4,2,32,256]{3,2,1,0:T(8,128)S(1)}, f32[4,2,32,256]{3,2,1,0:T(8,128)S(1)}, u32[]{:S(2)}, u32[]{:S(2)}) collective-permute-start(f32[4,2,32,256]{3,2,1,0:T(8,128)S(1)} %get-tuple-element.66), channel_id=1, source_target_pairs={{0,4},{4,8},{8,12},{1,5},{5,9},{9,13},{2,6},{6,10},{10,14},{3,7},{... | collective-permute-start | bytes 786440 | tf_op jit(solution)/shard_map/ppermute | solution.py:21
  9.1 4.2 %collective-permute-done = f32[4,2,32,256]{3,2,1,0:T(8,128)S(1)} collective-permute-done((f32[4,2,32,256]{3,2,1,0:T(8,128)S(1)}, f32[4,2,32,256]{3,2,1,0:T(8,128)S(1)}, u32[]{:S(2)}, u32[]{:S(2)}) %collective-permute-start) | collective-permute-done | bytes 262176 | tf_op jit(solution)/shard_map/ppermute | solution.py:21
  13.4 4.1 %collective-permute-done.1 = f32[4,2,32,256]{3,2,1,0:T(8,128)S(1)} collective-permute-done((f32[4,2,32,256]{3,2,1,0:T(8,128)S(1)}, f32[4,2,32,256]{3,2,1,0:T(8,128)S(1)}, u32[]{:S(2)}, u32[]{:S(2)}) %collective-permute-start.1) | collective-permute-done | bytes 262176 | tf_op jit(solution)/shard_map/ppermute | solution.py:24
  18.7 3.4 %collective-permute-start.2 = (f32[4,12,2,256]{3,2,1,0:T(2,128)S(1)}, f32[4,12,2,256]{3,2,1,0:T(2,128)S(1)}, u32[]{:S(2)}, u32[]{:S(2)}) collective-permute-start(f32[4,12,2,256]{3,2,1,0:T(2,128)S(1)} %get-tuple-element.58), channel_id=1, source_target_pairs={{0,2},{1,3},{4,6},{5,7},{8,10},{9,11},{12,14},{13,15},{16,18},{17,... | collective-permute-start | bytes 294920 | tf_op jit(solution)/shard_map/ppermute | solution.py:21
  24.3 4.3 %collective-permute-done.3 = f32[4,12,2,256]{3,2,1,0:T(2,128)S(1)} collective-permute-done((f32[4,12,2,256]{3,2,1,0:T(2,128)S(1)}, f32[4,12,2,256]{3,2,1,0:T(2,128)S(1)}, u32[]{:S(2)}, u32[]{:S(2)}) %collective-permute-start.3) | collective-permute-done | bytes 98336 | tf_op jit(solution)/shard_map/ppermute | solution.py:24
  34.1 2.2 copy.25
  37.6 2.2 copy.26
  39.8 2.2 copy.27
  42.0 3.1 %pad_maximum_fusion = f32[4,12,36,260]{3,2,1,0:T(8,128)S(1)} fusion(f32[4,12,36,2]{3,2,1,0:T(8,128)} %copy.27, f32[4,12,2,256]{3,2,1,0:T(2,128)} %copy-done.13, f32[4,2,32,256]{3,2,1,0:T(8,128)} %copy-done.5, f32[1,8,32,256]{3,2,1,0:T(8,128)S(1)} %multiply_bitcast_fusion, f32[3,8,32,256]{3,2,1,0:T(8,128)S(1)} %copy-done.1, ...), kind=kLoop, calls=%fused_computation.3 | loop fusion | flops 3144960 | bytes 3594240 | tf_op jit(solution)/shard_map/concatenate | solution.py:25
  45.3 2.2 multiply_multiply_fusion.5
  50.1 29.3 %fusion.51 = f32[1,8,32,256]{3,2,1,0:T(8,128)S(1)} fusion(f32[8,32,256]{2,1,0:T(8,128)S(1)} %copy-done.15, f32[12,36,260]{2,1,0:T(8,128)S(1)} %get-tuple-element.37, f32[10,34,258]{2,1,0:T(8,128)S(1)} %get-tuple-element.46, f32[10,34,258]{2,1,0:T(8,128)S(1)} %get-tuple-element.47, f32[10,34,258]{2,1,0:T(8,128)S(1)} %get-tuple-element.29, ...), kind=kLoop, calls=%fused_computation.127 | loop fusion | flops 23068672 | bytes 4194304 | tf_op jit(solution)/shard_map/broadcast_in_dim | solution.py:128
  80.3 3.5 %collective-permute-start.6 = (f32[4,2,32,256]{3,2,1,0:T(8,128)}, f32[4,2,32,256]{3,2,1,0:T(8,128)S(1)}, u32[]{:S(2)}, u32[]{:S(2)}) collective-permute-start(f32[4,2,32,256]{3,2,1,0:T(8,128)} %get-tuple-element.64), channel_id=1, source_target_pairs={{0,4},{4,8},{8,12},{1,5},{5,9},{9,13},{2,6},{6,10},{10,14},{3,7},{... | collective-permute-start | bytes 786440 | tf_op jit(solution)/shard_map/ppermute | solution.py:21
  85.7 4.3 %collective-permute-done.6 = f32[4,2,32,256]{3,2,1,0:T(8,128)S(1)} collective-permute-done((f32[4,2,32,256]{3,2,1,0:T(8,128)}, f32[4,2,32,256]{3,2,1,0:T(8,128)S(1)}, u32[]{:S(2)}, u32[]{:S(2)}) %collective-permute-start.6) | collective-permute-done | bytes 262176 | tf_op jit(solution)/shard_map/ppermute | solution.py:21
  90.0 4.7 %collective-permute-done.7 = f32[4,2,32,256]{3,2,1,0:T(8,128)} collective-permute-done((f32[4,2,32,256]{3,2,1,0:T(8,128)}, f32[4,2,32,256]{3,2,1,0:T(8,128)}, u32[]{:S(2)}, u32[]{:S(2)}) %collective-permute-start.7) | collective-permute-done | bytes 262176 | tf_op jit(solution)/shard_map/ppermute | solution.py:24
  100.0 4.1 %collective-permute-done.9 = f32[4,12,2,256]{3,2,1,0:T(2,128)S(1)} collective-permute-done((f32[4,12,2,256]{3,2,1,0:T(2,128)S(1)}, f32[4,12,2,256]{3,2,1,0:T(2,128)S(1)}, u32[]{:S(2)}, u32[]{:S(2)}) %collective-permute-start.9) | collective-permute-done | bytes 98336 | tf_op jit(solution)/shard_map/ppermute | solution.py:24
  108.8 1.9 collective-permute-start.10
  110.7 2.2 copy.29
  117.0 2.2 copy.30
  119.2 2.2 copy.31
  121.4 3.3 %pad_maximum_fusion.1 = f32[4,12,36,260]{3,2,1,0:T(8,128)S(1)} fusion(f32[4,12,36,2]{3,2,1,0:T(8,128)} %copy.31, f32[4,12,2,256]{3,2,1,0:T(2,128)} %copy-done.12, f32[4,2,32,256]{3,2,1,0:T(8,128)} %collective-permute-done.7, f32[1,8,32,256]{3,2,1,0:T(8,128)S(1)} %fusion.51, f32[3,8,32,256]{3,2,1,0:T(8,128)} %copy-done.2, ...), kind=kLoop, calls=%fused_computation.4 | loop fusion | flops 3144960 | bytes 3594240 | tf_op jit(solution)/shard_map/concatenate | solution.py:25
  124.9 3.8 %multiply_multiply_fusion.2 = (f32[10,34,258]{2,1,0:T(8,128)S(1)}, f32[10,34,258]{2,1,0:T(8,128)}, f32[10,34,258]{2,1,0:T(8,128)S(1)}, f32[10,34,258]{2,1,0:T(8,...) fusion(f32[12,36,260]{2,1,0:T(8,128)S(1)} %get-tuple-element.33, ...), kind=kLoop, calls=%fused_computation.61 | loop fusion | flops 2456160 | bytes 8421120 | tf_op jit(solution)/shard_map/mul | solution.py:106
  128.7 2.1 multiply_multiply_fusion
  135.0 60.5 %psum.7 = f32[3,4096]{1,0:T(4,128)} all-reduce(f32[3,4096]{1,0:T(4,128)} %fusion), channel_id=1, replica_groups=mesh['groups'=2,'slab'=4,'pencil'=2,'comp'=2] {'slab','pencil','comp'}, use_global_device_ids=true, to_apply=%region_1.0 | all-reduce | flops 12288 | bytes 98304 | tf_op jit(solution)/shard_map/psum | solution.py:144
  195.5 31.0 %fusion.26 = f32[8,32,256]{2,1,0:T(8,128)} fusion(f32[8,32,256]{2,1,0:T(8,128)} %param.6, f32[12,36,260]{2,1,0:T(8,128)S(1)} %copy-done.4, f32[10,34,258]{2,1,0:T(8,128)S(1)} %get-tuple-element.39, f32[10,34,258]{2,1,0:T(8,128)} %get-tuple-element.40, f32[10,34,258]{2,1,0:T(8,128)} %get-tuple-element.18, f32[10,34,258]{2,1,0:T(8,128)} %get-tuple-element.44, ...), kind=kLoop, calls=%fused_computation.82 | loop fusion | flops 23068672 | bytes 4194304 | tf_op jit(solution)/shard_map/add | solution.py:115
  (74 shorter events, 37.3 us)
Async XLA Ops:
  0.6 132.5 %copy-start = (bf16[8,32,1,4096]{3,1,2,0:T(8,128)(2,1)S(1)}, bf16[8,32,1,4096]{3,1,2,0:T(8,128)(2,1)}, u32[]{:S(2)}) copy-start(bf16[8,32,1,4096]{3,1,2,0:T(8,128)(2,1)} %param.8) | copy-start | bytes 6291460
  0.6 28.0 %copy-start.1 = (f32[3,8,32,256]{3,2,1,0:T(8,128)S(1)}, f32[3,8,32,256]{3,2,1,0:T(8,128)}, u32[]{:S(2)}) copy-start(f32[3,8,32,256]{3,2,1,0:T(8,128)} %param.5) | copy-start | bytes 2359300
  2.9 10.5 %collective-permute-start = (f32[4,2,32,256]{3,2,1,0:T(8,128)S(1)}, f32[4,2,32,256]{3,2,1,0:T(8,128)S(1)}, u32[]{:S(2)}, u32[]{:S(2)}) collective-permute-start(f32[4,2,32,256]{3,2,1,0:T(8,128)S(1)} %get-tuple-element.66), channel_id=1, source_target_pairs={{0,4},{4,8},{8,12},{1,5},{5,9},{9,13},{2,6},{6,10},{10,14},{3,7},{... | collective-permute-start | bytes 786440 | tf_op jit(solution)/shard_map/ppermute | solution.py:21
  7.8 9.7 %collective-permute-start.1 = (f32[4,2,32,256]{3,2,1,0:T(8,128)S(1)}, f32[4,2,32,256]{3,2,1,0:T(8,128)S(1)}, u32[]{:S(2)}, u32[]{:S(2)}) collective-permute-start(f32[4,2,32,256]{3,2,1,0:T(8,128)S(1)} %get-tuple-element.67), channel_id=1, source_target_pairs={{4,0},{8,4},{12,8},{5,1},{9,5},{13,9},{6,2},{10,6},{14,10},{7,3},{... | collective-permute-start | bytes 786440 | tf_op jit(solution)/shard_map/ppermute | solution.py:24
  17.5 13.0 %copy-start.5 = (f32[4,2,32,256]{3,2,1,0:T(8,128)}, f32[4,2,32,256]{3,2,1,0:T(8,128)S(1)}, u32[]{:S(2)}) copy-start(f32[4,2,32,256]{3,2,1,0:T(8,128)S(1)} %collective-permute-done.1) | copy-start | bytes 786436
  18.7 5.6 %collective-permute-start.2 = (f32[4,12,2,256]{3,2,1,0:T(2,128)S(1)}, f32[4,12,2,256]{3,2,1,0:T(2,128)S(1)}, u32[]{:S(2)}, u32[]{:S(2)}) collective-permute-start(f32[4,12,2,256]{3,2,1,0:T(2,128)S(1)} %get-tuple-element.58), channel_id=1, source_target_pairs={{0,2},{1,3},{4,6},{5,7},{8,10},{9,11},{12,14},{13,15},{16,18},{17,... | collective-permute-start | bytes 294920 | tf_op jit(solution)/shard_map/ppermute | solution.py:21
  22.1 6.5 %collective-permute-start.3 = (f32[4,12,2,256]{3,2,1,0:T(2,128)S(1)}, f32[4,12,2,256]{3,2,1,0:T(2,128)S(1)}, u32[]{:S(2)}, u32[]{:S(2)}) collective-permute-start(f32[4,12,2,256]{3,2,1,0:T(2,128)S(1)} %get-tuple-element.59), channel_id=1, source_target_pairs={{2,0},{3,1},{6,4},{7,5},{10,8},{11,9},{14,12},{15,13},{18,16},{19,... | collective-permute-start | bytes 294920 | tf_op jit(solution)/shard_map/ppermute | solution.py:24
  28.6 1.9 copy-start.13
  32.2 5.4 %collective-permute-start.4 = (f32[4,12,36,2]{2,0,3,1:T(4,128)S(1)}, f32[4,12,36,2]{2,0,3,1:T(4,128)}, u32[]{:S(2)}, u32[]{:S(2)}) collective-permute-start(f32[4,12,36,2]{2,0,3,1:T(4,128)S(1)} %copy.24), channel_id=1, source_target_pairs={{0,1},{2,3},{4,5},{6,7},{8,9},{10,11},{12,13},{14,15},{16,17},{18,... | collective-permute-start | bytes 41480 | tf_op jit(solution)/shard_map/ppermute | solution.py:21
  36.3 3.5 %collective-permute-start.5 = (f32[4,12,36,2]{2,0,3,1:T(4,128)}, f32[4,12,36,2]{2,0,3,1:T(4,128)}, u32[]{:S(2)}, u32[]{:S(2)}) collective-permute-start(f32[4,12,36,2]{2,0,3,1:T(4,128)} %copy.25), channel_id=1, source_target_pairs={{1,0},{3,2},{5,4},{7,6},{9,8},{11,10},{13,12},{15,14},{17,16},{19,... | collective-permute-start | bytes 41480 | tf_op jit(solution)/shard_map/ppermute | solution.py:24
  49.9 29.5 %copy-start.6 = (f32[1,8,32,256]{3,2,1,0:T(8,128)}, f32[1,8,32,256]{3,2,1,0:T(8,128)S(1)}, u32[]{:S(2)}) copy-start(f32[1,8,32,256]{3,2,1,0:T(8,128)S(1)} %get-tuple-element.71) | copy-start | bytes 786436
  49.9 29.5 %copy-start.8 = (f32[1,8,32,256]{3,2,1,0:T(8,128)}, f32[1,8,32,256]{3,2,1,0:T(8,128)S(1)}, u32[]{:S(2)}) copy-start(f32[1,8,32,256]{3,2,1,0:T(8,128)S(1)} %get-tuple-element.72) | copy-start | bytes 786436
  50.0 29.5 %copy-start.10 = (f32[1,8,32,256]{3,2,1,0:T(8,128)}, f32[1,8,32,256]{3,2,1,0:T(8,128)S(1)}, u32[]{:S(2)}) copy-start(f32[1,8,32,256]{3,2,1,0:T(8,128)S(1)} %get-tuple-element.73) | copy-start | bytes 786436
  50.1 30.2 %copy-start.2 = (f32[3,8,32,256]{3,2,1,0:T(8,128)}, f32[3,8,32,256]{3,2,1,0:T(8,128)S(1)}, u32[]{:S(2)}) copy-start(f32[3,8,32,256]{3,2,1,0:T(8,128)S(1)} %fusion.4) | copy-start | bytes 2359300
  80.3 9.7 %collective-permute-start.6 = (f32[4,2,32,256]{3,2,1,0:T(8,128)}, f32[4,2,32,256]{3,2,1,0:T(8,128)S(1)}, u32[]{:S(2)}, u32[]{:S(2)}) collective-permute-start(f32[4,2,32,256]{3,2,1,0:T(8,128)} %get-tuple-element.64), channel_id=1, source_target_pairs={{0,4},{4,8},{8,12},{1,5},{5,9},{9,13},{2,6},{6,10},{10,14},{3,7},{... | collective-permute-start | bytes 786440 | tf_op jit(solution)/shard_map/ppermute | solution.py:21
  83.8 10.9 %collective-permute-start.7 = (f32[4,2,32,256]{3,2,1,0:T(8,128)}, f32[4,2,32,256]{3,2,1,0:T(8,128)}, u32[]{:S(2)}, u32[]{:S(2)}) collective-permute-start(f32[4,2,32,256]{3,2,1,0:T(8,128)} %get-tuple-element.65), channel_id=1, source_target_pairs={{4,0},{8,4},{12,8},{5,1},{9,5},{13,9},{6,2},{10,6},{14,10},{7,3},{... | collective-permute-start | bytes 786440 | tf_op jit(solution)/shard_map/ppermute | solution.py:24
  95.9 4.1 %collective-permute-start.8 = (f32[4,12,2,256]{3,2,1,0:T(2,128)S(1)}, f32[4,12,2,256]{3,2,1,0:T(2,128)S(1)}, u32[]{:S(2)}, u32[]{:S(2)}) collective-permute-start(f32[4,12,2,256]{3,2,1,0:T(2,128)S(1)} %get-tuple-element.56), channel_id=1, source_target_pairs={{0,2},{1,3},{4,6},{5,7},{8,10},{9,11},{12,14},{13,15},{16,18},{17,... | collective-permute-start | bytes 294920 | tf_op jit(solution)/shard_map/ppermute | solution.py:21
  97.4 6.7 %collective-permute-start.9 = (f32[4,12,2,256]{3,2,1,0:T(2,128)S(1)}, f32[4,12,2,256]{3,2,1,0:T(2,128)S(1)}, u32[]{:S(2)}, u32[]{:S(2)}) collective-permute-start(f32[4,12,2,256]{3,2,1,0:T(2,128)S(1)} %get-tuple-element.57), channel_id=1, source_target_pairs={{2,0},{3,1},{6,4},{7,5},{10,8},{11,9},{14,12},{15,13},{18,16},{19,... | collective-permute-start | bytes 294920 | tf_op jit(solution)/shard_map/ppermute | solution.py:24
  104.1 3.1 %copy-start.12 = (f32[4,12,2,256]{3,2,1,0:T(2,128)}, f32[4,12,2,256]{3,2,1,0:T(2,128)S(1)}, u32[]{:S(2)}) copy-start(f32[4,12,2,256]{3,2,1,0:T(2,128)S(1)} %collective-permute-done.9) | copy-start | bytes 294916
  108.8 8.1 %collective-permute-start.10 = (f32[4,12,36,2]{2,0,3,1:T(4,128)S(1)}, f32[4,12,36,2]{2,0,3,1:T(4,128)}, u32[]{:S(2)}, u32[]{:S(2)}) collective-permute-start(f32[4,12,36,2]{2,0,3,1:T(4,128)S(1)} %copy.28), channel_id=1, source_target_pairs={{0,1},{2,3},{4,5},{6,7},{8,9},{10,11},{12,13},{14,15},{16,17},{18,... | collective-permute-start | bytes 41480 | tf_op jit(solution)/shard_map/ppermute | solution.py:21
  113.0 6.2 %collective-permute-start.11 = (f32[4,12,36,2]{2,0,3,1:T(4,128)}, f32[4,12,36,2]{2,0,3,1:T(4,128)}, u32[]{:S(2)}, u32[]{:S(2)}) collective-permute-start(f32[4,12,36,2]{2,0,3,1:T(4,128)} %copy.29), channel_id=1, source_target_pairs={{1,0},{3,2},{5,4},{7,6},{9,8},{11,10},{13,12},{15,14},{17,16},{19,... | collective-permute-start | bytes 41480 | tf_op jit(solution)/shard_map/ppermute | solution.py:24
  124.9 3.8 %copy-start.3 = (f32[12,36,260]{2,1,0:T(8,128)}, f32[12,36,260]{2,1,0:T(8,128)S(1)}, u32[]{:S(2)}) copy-start(f32[12,36,260]{2,1,0:T(8,128)S(1)} %get-tuple-element.33) | copy-start | bytes 1347844
  132.0 1.6 copy-start.14
  133.1 62.5 %copy-start.4 = (f32[12,36,260]{2,1,0:T(8,128)S(1)}, f32[12,36,260]{2,1,0:T(8,128)}, u32[]{:S(2)}) copy-start(f32[12,36,260]{2,1,0:T(8,128)} %copy-done.3) | copy-start | bytes 1347844
  (5 other events, 6.4 us)
where the time goes:
time: 228 us; the launch traced here: 227 us
  other arithmetic  89.2 us (39%)
  blocking collectives  60.5 us (27%)
  waiting for transfers between devices  27.4 us (12%)
  starting transfers between devices  24.9 us (11%)
  local copies, waits for them, and re-layouts  21.7 us (10%)
    psum x1, blocking collectives, local(): readings = lax.psum(partial_sum, ('slab', 'pencil', 'comp'))  60.5 us
    add x1, other arithmetic, advance(): damage_core + TIME_DAMAGE * (2.0 * (1.0 - damage_core) * energy - toughne...  31 us
    broadcast_in_dim x2, other arithmetic, local(): stacked = jnp.concatenate([moved, damage[None]], axis=0)  30.5 us
    ppermute x6, waiting for transfers between devices, with_halo(): lax.ppermute(lax.slice_in_dim(block, 0, width, axis=dim), axis, backward)  17.3 us
    ppermute x6, starting transfers between devices, with_halo(): lax.ppermute(lax.slice_in_dim(block, block.shape[dim] - width, None, axis...  17.2 us
    ppermute x6, waiting for transfers between devices, with_halo(): lax.ppermute(lax.slice_in_dim(block, block.shape[dim] - width, None, axis...  10.2 us
    mul x4, other arithmetic, advance(): total_force = total_force + central(degrade * stress, direction)  9.3 us
    concatenate x4, other arithmetic, with_halo(): block = jnp.concatenate([low, block, high], axis=dim)  8.23 us
  transfers between devices with their start and end apart: 12, of which 8 were waited for; matrix products, arithmetic and copies ran while one was open for 6% of the time, Pallas kernels for 0%

commit v1 on v0

--- a/solution.py
+++ b/solution.py
@@ -141,7 +141,7 @@
     picks = (block_ids[:, None] == sensor_cell[None, :]).astype(jnp.bfloat16)
     point = jnp.dot(pooled, picks, preferred_element_type=jnp.float32)
     partial_sum = dense + POINT_GAIN * point
-    readings = lax.psum(partial_sum, ("slab", "pencil", "comp"))
+    readings = jnp.sum(lax.all_gather(partial_sum, ("slab", "pencil", "comp")), axis=0)
     return (moved, damage, readings)
 
 

time: 228 us -> 192 us (0.84)
  blocking collectives: 60.5 us -> 23.5 us
    psum x1 -> x0, blocking collectives: 60.5 us -> none  [local(): readings = lax.psum(partial_sum, ('slab', 'pencil', 'comp'))]
    all_gather x0 -> x1, blocking collectives: none -> 23.5 us  [local(): lax.all_gather(partial_sum, ('slab', 'pencil', 'comp'))]
  transfers between devices with their start and end apart: 12 -> 12, of which waited for: 8 -> 8; matrix products, arithmetic and copies ran while one was open for 6% -> 7% of each run, Pallas kernels for 0% -> 0%
where the time goes in v1:
time: 192 us; the launch traced here: 191 us
  other arithmetic  91.3 us (48%)
  waiting for transfers between devices  27.4 us (14%)
  starting transfers between devices  24.9 us (13%)
  blocking collectives  23.5 us (12%)
  local copies, waits for them, and re-layouts  21.7 us (11%)
    add x1, other arithmetic, advance(): damage_core + TIME_DAMAGE * (2.0 * (1.0 - damage_core) * energy - toughne...  31 us
    broadcast_in_dim x2, other arithmetic, local(): stacked = jnp.concatenate([moved, damage[None]], axis=0)  30.5 us
    all_gather x1, blocking collectives, local(): lax.all_gather(partial_sum, ('slab', 'pencil', 'comp'))  23.5 us
    ppermute x6, waiting for transfers between devices, with_halo(): lax.ppermute(lax.slice_in_dim(block, 0, width, axis=dim), axis, backward)  17.3 us
    ppermute x6, starting transfers between devices, with_halo(): lax.ppermute(lax.slice_in_dim(block, block.shape[dim] - width, None, axis...  17.2 us
    ppermute x6, waiting for transfers between devices, with_halo(): lax.ppermute(lax.slice_in_dim(block, block.shape[dim] - width, None, axis...  10.1 us
    mul x4, other arithmetic, advance(): total_force = total_force + central(degrade * stress, direction)  9.34 us
    concatenate x4, other arithmetic, with_halo(): block = jnp.concatenate([low, block, high], axis=dim)  8.23 us
  transfers between devices with their start and end apart: 12, of which 8 were waited for; matrix products, arithmetic and copies ran while one was open for 7% of the time, Pallas kernels for 0%

profile of v1, /device:TPU:0, one launch (start us, length us, event | category | flops | bytes accessed | tf_op | source)
XLA Modules:
  0.0 190.9 jit_solution(16494714979199537831)
XLA Ops:
  2.9 5.0 %collective-permute-start = (f32[4,2,32,256]{3,2,1,0:T(8,128)S(1)}, f32[4,2,32,256]{3,2,1,0:T(8,128)S(1)}, u32[]{:S(2)}, u32[]{:S(2)}) collective-permute-start(f32[4,2,32,256]{3,2,1,0:T(8,128)S(1)} %get-tuple-element.66), channel_id=1, source_target_pairs={{0,4},{4,8},{8,12},{1,5},{5,9},{9,13},{2,6},{6,10},{10,14},{3,7},{... | collective-permute-start | bytes 786440 | tf_op jit(solution)/shard_map/ppermute | solution.py:21
  9.1 4.2 %collective-permute-done = f32[4,2,32,256]{3,2,1,0:T(8,128)S(1)} collective-permute-done((f32[4,2,32,256]{3,2,1,0:T(8,128)S(1)}, f32[4,2,32,256]{3,2,1,0:T(8,128)S(1)}, u32[]{:S(2)}, u32[]{:S(2)}) %collective-permute-start) | collective-permute-done | bytes 262176 | tf_op jit(solution)/shard_map/ppermute | solution.py:21
  13.4 4.1 %collective-permute-done.1 = f32[4,2,32,256]{3,2,1,0:T(8,128)S(1)} collective-permute-done((f32[4,2,32,256]{3,2,1,0:T(8,128)S(1)}, f32[4,2,32,256]{3,2,1,0:T(8,128)S(1)}, u32[]{:S(2)}, u32[]{:S(2)}) %collective-permute-start.1) | collective-permute-done | bytes 262176 | tf_op jit(solution)/shard_map/ppermute | solution.py:24
  18.7 3.4 %collective-permute-start.2 = (f32[4,12,2,256]{3,2,1,0:T(2,128)S(1)}, f32[4,12,2,256]{3,2,1,0:T(2,128)S(1)}, u32[]{:S(2)}, u32[]{:S(2)}) collective-permute-start(f32[4,12,2,256]{3,2,1,0:T(2,128)S(1)} %get-tuple-element.58), channel_id=1, source_target_pairs={{0,2},{1,3},{4,6},{5,7},{8,10},{9,11},{12,14},{13,15},{16,18},{17,... | collective-permute-start | bytes 294920 | tf_op jit(solution)/shard_map/ppermute | solution.py:21
  24.3 4.3 %collective-permute-done.3 = f32[4,12,2,256]{3,2,1,0:T(2,128)S(1)} collective-permute-done((f32[4,12,2,256]{3,2,1,0:T(2,128)S(1)}, f32[4,12,2,256]{3,2,1,0:T(2,128)S(1)}, u32[]{:S(2)}, u32[]{:S(2)}) %collective-permute-start.3) | collective-permute-done | bytes 98336 | tf_op jit(solution)/shard_map/ppermute | solution.py:24
  34.1 2.2 %copy.25 = f32[4,12,36,2]{2,0,3,1:T(4,128)} copy(f32[4,12,36,2]{3,2,1,0:T(8,128)} %get-tuple-element.55) | data formatting | bytes 27648 | tf_op jit(solution)/shard_map/slice | solution.py:24
  37.6 2.2 %copy.26 = f32[4,12,36,2]{3,2,1,0:T(8,128)} copy(f32[4,12,36,2]{2,0,3,1:T(4,128)} %collective-permute-done.4) | data formatting | bytes 27648 | tf_op jit(solution)/shard_map/ppermute | solution.py:21
  39.8 2.2 %copy.27 = f32[4,12,36,2]{3,2,1,0:T(8,128)} copy(f32[4,12,36,2]{2,0,3,1:T(4,128)} %collective-permute-done.5) | data formatting | bytes 27648 | tf_op jit(solution)/shard_map/ppermute | solution.py:24
  42.0 3.1 %pad_maximum_fusion = f32[4,12,36,260]{3,2,1,0:T(8,128)S(1)} fusion(f32[4,12,36,2]{3,2,1,0:T(8,128)} %copy.27, f32[4,12,2,256]{3,2,1,0:T(2,128)} %copy-done.13, f32[4,2,32,256]{3,2,1,0:T(8,128)} %copy-done.5, f32[1,8,32,256]{3,2,1,0:T(8,128)S(1)} %multiply_bitcast_fusion, f32[3,8,32,256]{3,2,1,0:T(8,128)S(1)} %copy-done.1, ...), kind=kLoop, calls=%fused_computation.4 | loop fusion | flops 3144960 | bytes 3594240 | tf_op jit(solution)/shard_map/concatenate | solution.py:25
  45.3 2.2 %multiply_multiply_fusion.5 = (f32[10,34,258]{2,1,0:T(8,128)S(1)}, f32[10,34,258]{2,1,0:T(8,128)S(1)}, f32[10,34,258]{2,1,0:T(8,128)S(1)}, f32[10,34,258]{2,1,0:...) fusion(f32[12,36,260]{2,1,0:T(8,128)S(1)} %get-tuple-element.37, ...), kind=kLoop, calls=%fused_computation.69 | loop fusion | flops 2456160 | bytes 8421120 | tf_op jit(solution)/shard_map/mul | solution.py:106
  50.1 29.3 %fusion.52 = f32[1,8,32,256]{3,2,1,0:T(8,128)S(1)} fusion(f32[8,32,256]{2,1,0:T(8,128)S(1)} %copy-done.15, f32[12,36,260]{2,1,0:T(8,128)S(1)} %get-tuple-element.37, f32[10,34,258]{2,1,0:T(8,128)S(1)} %get-tuple-element.46, f32[10,34,258]{2,1,0:T(8,128)S(1)} %get-tuple-element.47, f32[10,34,258]{2,1,0:T(8,128)S(1)} %get-tuple-element.29, ...), kind=kLoop, calls=%fused_computation.128 | loop fusion | flops 23068672 | bytes 4194304 | tf_op jit(solution)/shard_map/broadcast_in_dim | solution.py:128
  80.3 3.5 %collective-permute-start.6 = (f32[4,2,32,256]{3,2,1,0:T(8,128)}, f32[4,2,32,256]{3,2,1,0:T(8,128)S(1)}, u32[]{:S(2)}, u32[]{:S(2)}) collective-permute-start(f32[4,2,32,256]{3,2,1,0:T(8,128)} %get-tuple-element.64), channel_id=1, source_target_pairs={{0,4},{4,8},{8,12},{1,5},{5,9},{9,13},{2,6},{6,10},{10,14},{3,7},{... | collective-permute-start | bytes 786440 | tf_op jit(solution)/shard_map/ppermute | solution.py:21
  85.7 4.3 %collective-permute-done.6 = f32[4,2,32,256]{3,2,1,0:T(8,128)S(1)} collective-permute-done((f32[4,2,32,256]{3,2,1,0:T(8,128)}, f32[4,2,32,256]{3,2,1,0:T(8,128)S(1)}, u32[]{:S(2)}, u32[]{:S(2)}) %collective-permute-start.6) | collective-permute-done | bytes 262176 | tf_op jit(solution)/shard_map/ppermute | solution.py:21
  90.0 4.7 %collective-permute-done.7 = f32[4,2,32,256]{3,2,1,0:T(8,128)} collective-permute-done((f32[4,2,32,256]{3,2,1,0:T(8,128)}, f32[4,2,32,256]{3,2,1,0:T(8,128)}, u32[]{:S(2)}, u32[]{:S(2)}) %collective-permute-start.7) | collective-permute-done | bytes 262176 | tf_op jit(solution)/shard_map/ppermute | solution.py:24
  100.0 4.1 %collective-permute-done.9 = f32[4,12,2,256]{3,2,1,0:T(2,128)S(1)} collective-permute-done((f32[4,12,2,256]{3,2,1,0:T(2,128)S(1)}, f32[4,12,2,256]{3,2,1,0:T(2,128)S(1)}, u32[]{:S(2)}, u32[]{:S(2)}) %collective-permute-start.9) | collective-permute-done | bytes 98336 | tf_op jit(solution)/shard_map/ppermute | solution.py:24
  110.7 2.2 %copy.29 = f32[4,12,36,2]{2,0,3,1:T(4,128)} copy(f32[4,12,36,2]{3,2,1,0:T(8,128)} %get-tuple-element.53) | data formatting | bytes 27648 | tf_op jit(solution)/shard_map/slice | solution.py:24
  116.9 2.2 %copy.30 = f32[4,12,36,2]{3,2,1,0:T(8,128)} copy(f32[4,12,36,2]{2,0,3,1:T(4,128)} %collective-permute-done.10) | data formatting | bytes 27648 | tf_op jit(solution)/shard_map/ppermute | solution.py:21
  119.1 2.2 %copy.31 = f32[4,12,36,2]{3,2,1,0:T(8,128)} copy(f32[4,12,36,2]{2,0,3,1:T(4,128)} %collective-permute-done.11) | data formatting | bytes 27648 | tf_op jit(solution)/shard_map/ppermute | solution.py:24
  121.3 3.3 %pad_maximum_fusion.1 = f32[4,12,36,260]{3,2,1,0:T(8,128)S(1)} fusion(f32[4,12,36,2]{3,2,1,0:T(8,128)} %copy.31, f32[4,12,2,256]{3,2,1,0:T(2,128)} %copy-done.12, f32[4,2,32,256]{3,2,1,0:T(8,128)} %collective-permute-done.7, f32[1,8,32,256]{3,2,1,0:T(8,128)S(1)} %fusion.52, f32[3,8,32,256]{3,2,1,0:T(8,128)} %copy-done.2, ...), kind=kLoop, calls=%fused_computation.5 | loop fusion | flops 3144960 | bytes 3594240 | tf_op jit(solution)/shard_map/concatenate | solution.py:25
  124.9 3.8 %multiply_multiply_fusion.2 = (f32[10,34,258]{2,1,0:T(8,128)S(1)}, f32[10,34,258]{2,1,0:T(8,128)}, f32[10,34,258]{2,1,0:T(8,128)S(1)}, f32[10,34,258]{2,1,0:T(8,...) fusion(f32[12,36,260]{2,1,0:T(8,128)S(1)} %get-tuple-element.33, ...), kind=kLoop, calls=%fused_computation.62 | loop fusion | flops 2456160 | bytes 8421120 | tf_op jit(solution)/shard_map/mul | solution.py:106
  128.7 2.1 %multiply_multiply_fusion = (f32[10,34,258]{2,1,0:T(8,128)S(1)}, f32[10,34,258]{2,1,0:T(8,128)}, f32[10,34,258]{2,1,0:T(8,128)S(1)}, f32[10,34,258]{2,1,0:T(8,128)S(1)}) fusion(f32[12,36,260]{2,1,0:T(8,128)S(1)} %get-tuple-element.33, f32[12,36,260]{2,1,0:T(8,128)S(1)} %get-tuple-element.30, f32[12,36,260]{2,1,0:T(8,128)S(1)} %get-tuple-element.31, ...), kind=kLoop, calls=%fused_computation.59 | loop fusion | flops 1666680 | bytes 4912320 | tf_op jit(solution)/shard_map/mul | solution.py:106
  134.4 23.5 %all-gather.1 = f32[16,3,4096]{2,1,0:T(4,128)} all-gather(f32[1,3,4096]{2,1,0:T(4,128)S(1)} %fusion.1), channel_id=2, replica_groups=mesh['groups'=2,'slab'=4,'pencil'=2,'comp'=2] {'slab','pencil','comp'}, dimensions={0}, use_global_device_ids=true | all-gather | bytes 835584 | tf_op jit(solution)/shard_map/all_gather | solution.py:144
  157.8 2.0 %reduce_sum.19 = f32[3,4096]{1,0:T(4,128)} reduce(f32[16,3,4096]{2,1,0:T(4,128)} %all-gather.1, f32[]{:T(128)} %constant.62.clone.1), dimensions={0}, to_apply=%region_1.0 | reduce | flops 184320 | bytes 835588 | tf_op jit(solution)/shard_map/reduce_sum | solution.py:144
  159.8 31.0 %fusion.27 = f32[8,32,256]{2,1,0:T(8,128)} fusion(f32[8,32,256]{2,1,0:T(8,128)} %param.6, f32[12,36,260]{2,1,0:T(8,128)S(1)} %copy-done.4, f32[10,34,258]{2,1,0:T(8,128)S(1)} %get-tuple-element.39, f32[10,34,258]{2,1,0:T(8,128)} %get-tuple-element.40, f32[10,34,258]{2,1,0:T(8,128)} %get-tuple-element.18, f32[10,34,258]{2,1,0:T(8,128)} %get-tuple-element.44, ...), kind=kLoop, calls=%fused_computation.83 | loop fusion | flops 23068672 | bytes 4194304 | tf_op jit(solution)/shard_map/add | solution.py:115
  (75 shorter events, 38.5 us)
Async XLA Ops:
  0.6 132.5 %copy-start = (bf16[8,32,1,4096]{3,1,2,0:T(8,128)(2,1)S(1)}, bf16[8,32,1,4096]{3,1,2,0:T(8,128)(2,1)}, u32[]{:S(2)}) copy-start(bf16[8,32,1,4096]{3,1,2,0:T(8,128)(2,1)} %param.8) | copy-start | bytes 6291460
  0.6 28.0 %copy-start.1 = (f32[3,8,32,256]{3,2,1,0:T(8,128)S(1)}, f32[3,8,32,256]{3,2,1,0:T(8,128)}, u32[]{:S(2)}) copy-start(f32[3,8,32,256]{3,2,1,0:T(8,128)} %param.5) | copy-start | bytes 2359300
  2.9 10.5 %collective-permute-start = (f32[4,2,32,256]{3,2,1,0:T(8,128)S(1)}, f32[4,2,32,256]{3,2,1,0:T(8,128)S(1)}, u32[]{:S(2)}, u32[]{:S(2)}) collective-permute-start(f32[4,2,32,256]{3,2,1,0:T(8,128)S(1)} %get-tuple-element.66), channel_id=1, source_target_pairs={{0,4},{4,8},{8,12},{1,5},{5,9},{9,13},{2,6},{6,10},{10,14},{3,7},{... | collective-permute-start | bytes 786440 | tf_op jit(solution)/shard_map/ppermute | solution.py:21
  7.8 9.7 %collective-permute-start.1 = (f32[4,2,32,256]{3,2,1,0:T(8,128)S(1)}, f32[4,2,32,256]{3,2,1,0:T(8,128)S(1)}, u32[]{:S(2)}, u32[]{:S(2)}) collective-permute-start(f32[4,2,32,256]{3,2,1,0:T(8,128)S(1)} %get-tuple-element.67), channel_id=1, source_target_pairs={{4,0},{8,4},{12,8},{5,1},{9,5},{13,9},{6,2},{10,6},{14,10},{7,3},{... | collective-permute-start | bytes 786440 | tf_op jit(solution)/shard_map/ppermute | solution.py:24
  17.5 13.0 %copy-start.5 = (f32[4,2,32,256]{3,2,1,0:T(8,128)}, f32[4,2,32,256]{3,2,1,0:T(8,128)S(1)}, u32[]{:S(2)}) copy-start(f32[4,2,32,256]{3,2,1,0:T(8,128)S(1)} %collective-permute-done.1) | copy-start | bytes 786436
  18.7 5.6 %collective-permute-start.2 = (f32[4,12,2,256]{3,2,1,0:T(2,128)S(1)}, f32[4,12,2,256]{3,2,1,0:T(2,128)S(1)}, u32[]{:S(2)}, u32[]{:S(2)}) collective-permute-start(f32[4,12,2,256]{3,2,1,0:T(2,128)S(1)} %get-tuple-element.58), channel_id=1, source_target_pairs={{0,2},{1,3},{4,6},{5,7},{8,10},{9,11},{12,14},{13,15},{16,18},{17,... | collective-permute-start | bytes 294920 | tf_op jit(solution)/shard_map/ppermute | solution.py:21
  22.1 6.5 %collective-permute-start.3 = (f32[4,12,2,256]{3,2,1,0:T(2,128)S(1)}, f32[4,12,2,256]{3,2,1,0:T(2,128)S(1)}, u32[]{:S(2)}, u32[]{:S(2)}) collective-permute-start(f32[4,12,2,256]{3,2,1,0:T(2,128)S(1)} %get-tuple-element.59), channel_id=1, source_target_pairs={{2,0},{3,1},{6,4},{7,5},{10,8},{11,9},{14,12},{15,13},{18,16},{19,... | collective-permute-start | bytes 294920 | tf_op jit(solution)/shard_map/ppermute | solution.py:24
  28.6 1.9 %copy-start.13 = (f32[4,12,2,256]{3,2,1,0:T(2,128)}, f32[4,12,2,256]{3,2,1,0:T(2,128)S(1)}, u32[]{:S(2)}) copy-start(f32[4,12,2,256]{3,2,1,0:T(2,128)S(1)} %collective-permute-done.3) | copy-start | bytes 294916
  32.2 5.4 %collective-permute-start.4 = (f32[4,12,36,2]{2,0,3,1:T(4,128)S(1)}, f32[4,12,36,2]{2,0,3,1:T(4,128)}, u32[]{:S(2)}, u32[]{:S(2)}) collective-permute-start(f32[4,12,36,2]{2,0,3,1:T(4,128)S(1)} %copy.24), channel_id=1, source_target_pairs={{0,1},{2,3},{4,5},{6,7},{8,9},{10,11},{12,13},{14,15},{16,17},{18,... | collective-permute-start | bytes 41480 | tf_op jit(solution)/shard_map/ppermute | solution.py:21
  36.3 3.5 %collective-permute-start.5 = (f32[4,12,36,2]{2,0,3,1:T(4,128)}, f32[4,12,36,2]{2,0,3,1:T(4,128)}, u32[]{:S(2)}, u32[]{:S(2)}) collective-permute-start(f32[4,12,36,2]{2,0,3,1:T(4,128)} %copy.25), channel_id=1, source_target_pairs={{1,0},{3,2},{5,4},{7,6},{9,8},{11,10},{13,12},{15,14},{17,16},{19,... | collective-permute-start | bytes 41480 | tf_op jit(solution)/shard_map/ppermute | solution.py:24
  49.9 29.5 %copy-start.6 = (f32[1,8,32,256]{3,2,1,0:T(8,128)}, f32[1,8,32,256]{3,2,1,0:T(8,128)S(1)}, u32[]{:S(2)}) copy-start(f32[1,8,32,256]{3,2,1,0:T(8,128)S(1)} %get-tuple-element.71) | copy-start | bytes 786436
  50.0 29.5 %copy-start.8 = (f32[1,8,32,256]{3,2,1,0:T(8,128)}, f32[1,8,32,256]{3,2,1,0:T(8,128)S(1)}, u32[]{:S(2)}) copy-start(f32[1,8,32,256]{3,2,1,0:T(8,128)S(1)} %get-tuple-element.72) | copy-start | bytes 786436
  50.0 29.5 %copy-start.10 = (f32[1,8,32,256]{3,2,1,0:T(8,128)}, f32[1,8,32,256]{3,2,1,0:T(8,128)S(1)}, u32[]{:S(2)}) copy-start(f32[1,8,32,256]{3,2,1,0:T(8,128)S(1)} %get-tuple-element.73) | copy-start | bytes 786436
  50.1 30.2 %copy-start.2 = (f32[3,8,32,256]{3,2,1,0:T(8,128)}, f32[3,8,32,256]{3,2,1,0:T(8,128)S(1)}, u32[]{:S(2)}) copy-start(f32[3,8,32,256]{3,2,1,0:T(8,128)S(1)} %fusion.5) | copy-start | bytes 2359300
  80.3 9.7 %collective-permute-start.6 = (f32[4,2,32,256]{3,2,1,0:T(8,128)}, f32[4,2,32,256]{3,2,1,0:T(8,128)S(1)}, u32[]{:S(2)}, u32[]{:S(2)}) collective-permute-start(f32[4,2,32,256]{3,2,1,0:T(8,128)} %get-tuple-element.64), channel_id=1, source_target_pairs={{0,4},{4,8},{8,12},{1,5},{5,9},{9,13},{2,6},{6,10},{10,14},{3,7},{... | collective-permute-start | bytes 786440 | tf_op jit(solution)/shard_map/ppermute | solution.py:21
  83.8 10.9 %collective-permute-start.7 = (f32[4,2,32,256]{3,2,1,0:T(8,128)}, f32[4,2,32,256]{3,2,1,0:T(8,128)}, u32[]{:S(2)}, u32[]{:S(2)}) collective-permute-start(f32[4,2,32,256]{3,2,1,0:T(8,128)} %get-tuple-element.65), channel_id=1, source_target_pairs={{4,0},{8,4},{12,8},{5,1},{9,5},{13,9},{6,2},{10,6},{14,10},{7,3},{... | collective-permute-start | bytes 786440 | tf_op jit(solution)/shard_map/ppermute | solution.py:24
  95.9 4.1 %collective-permute-start.8 = (f32[4,12,2,256]{3,2,1,0:T(2,128)S(1)}, f32[4,12,2,256]{3,2,1,0:T(2,128)S(1)}, u32[]{:S(2)}, u32[]{:S(2)}) collective-permute-start(f32[4,12,2,256]{3,2,1,0:T(2,128)S(1)} %get-tuple-element.56), channel_id=1, source_target_pairs={{0,2},{1,3},{4,6},{5,7},{8,10},{9,11},{12,14},{13,15},{16,18},{17,... | collective-permute-start | bytes 294920 | tf_op jit(solution)/shard_map/ppermute | solution.py:21
  97.4 6.6 %collective-permute-start.9 = (f32[4,12,2,256]{3,2,1,0:T(2,128)S(1)}, f32[4,12,2,256]{3,2,1,0:T(2,128)S(1)}, u32[]{:S(2)}, u32[]{:S(2)}) collective-permute-start(f32[4,12,2,256]{3,2,1,0:T(2,128)S(1)} %get-tuple-element.57), channel_id=1, source_target_pairs={{2,0},{3,1},{6,4},{7,5},{10,8},{11,9},{14,12},{15,13},{18,16},{19,... | collective-permute-start | bytes 294920 | tf_op jit(solution)/shard_map/ppermute | solution.py:24
  104.1 3.1 %copy-start.12 = (f32[4,12,2,256]{3,2,1,0:T(2,128)}, f32[4,12,2,256]{3,2,1,0:T(2,128)S(1)}, u32[]{:S(2)}) copy-start(f32[4,12,2,256]{3,2,1,0:T(2,128)S(1)} %collective-permute-done.9) | copy-start | bytes 294916
  108.8 8.1 %collective-permute-start.10 = (f32[4,12,36,2]{2,0,3,1:T(4,128)S(1)}, f32[4,12,36,2]{2,0,3,1:T(4,128)}, u32[]{:S(2)}, u32[]{:S(2)}) collective-permute-start(f32[4,12,36,2]{2,0,3,1:T(4,128)S(1)} %copy.28), channel_id=1, source_target_pairs={{0,1},{2,3},{4,5},{6,7},{8,9},{10,11},{12,13},{14,15},{16,17},{18,... | collective-permute-start | bytes 41480 | tf_op jit(solution)/shard_map/ppermute | solution.py:21
  112.9 6.2 %collective-permute-start.11 = (f32[4,12,36,2]{2,0,3,1:T(4,128)}, f32[4,12,36,2]{2,0,3,1:T(4,128)}, u32[]{:S(2)}, u32[]{:S(2)}) collective-permute-start(f32[4,12,36,2]{2,0,3,1:T(4,128)} %copy.29), channel_id=1, source_target_pairs={{1,0},{3,2},{5,4},{7,6},{9,8},{11,10},{13,12},{15,14},{17,16},{19,... | collective-permute-start | bytes 41480 | tf_op jit(solution)/shard_map/ppermute | solution.py:24
  124.9 3.8 %copy-start.3 = (f32[12,36,260]{2,1,0:T(8,128)}, f32[12,36,260]{2,1,0:T(8,128)S(1)}, u32[]{:S(2)}) copy-start(f32[12,36,260]{2,1,0:T(8,128)S(1)} %get-tuple-element.33) | copy-start | bytes 1347844
  132.0 1.6 copy-start.14
  133.1 26.8 %copy-start.4 = (f32[12,36,260]{2,1,0:T(8,128)S(1)}, f32[12,36,260]{2,1,0:T(8,128)}, u32[]{:S(2)}) copy-start(f32[12,36,260]{2,1,0:T(8,128)} %copy-done.3) | copy-start | bytes 1347844
  (5 other events, 6.4 us)
